TPU v7x, 32 devices: a whole 2x2x4 slice. The times are simulated.
32 devices in a mesh: seq: 8 (over z, x), head: 4 (over y, core).
Axes of the slice: x: 2, y: 2, z: 4, core: 2. Of those that a mesh axis runs over, the one named last changes fastest.
Arguments:
- patches: bfloat16 [32768, 768], P('seq'), may hold values from -6 to 6
- slot_image: int32 [128], P('seq'), may hold values from -1 to 63, as said below
- slot_dest: int32 [128], P('seq'), may hold values from -1 to 63, as said below
- enc_gain: float32 [768], replicated, may hold values from 0.1 to 1.9
- w_qkv: bfloat16 [3, 768, 768], P(None, None, 'head'), may hold values from -1.2 to 1.2
- w_out: bfloat16 [768, 768], P('head'), may hold values from -0.21875 to 0.21875
- fast_gain: float32 [768], replicated, may hold values from 0.1 to 1.9
- w_fast: bfloat16 [3, 768, 768], P(None, None, 'head'), may hold values from -0.21875 to 0.21875
- w_rate: bfloat16 [768, 4], P(None, 'head'), may hold values from -0.21875 to 0.21875
- fast_gate_up: float32 [4, 2, 192, 384], P('head'), may hold values from -0.4375 to 0.4375
- fast_down: float32 [4, 384, 192], P('head'), may hold values from -0.3125 to 0.3125
Outputs:
- view_out: bfloat16 [16384, 768], P('seq', 'head')
Inputs may be any that keep to these rules, and one draw needn't show every extreme that they name: slot_dest gives for each slot the view-order block that its block becomes, or -1 for an empty slot; every view-order block is named by exactly one slot. Slots 2i and 2i + 1 of one seq index are both empty or name view blocks 2m and 2m + 1. The slots of one seq index name at most 2 blocks of any one view shard (blocks s * 8 to (s + 1) * 8 - 1), and some seq index uses all of its slots. slot_image is -1 exactly where slot_dest is -1; an image is one block or the two blocks of a slot pair, and different images have different ids.
All inputs are finite; a program needn't handle non-finite values.
Results may differ from a plain program's by a relative error of at most 0.035.
Values may be sent and summed in bfloat16 or wider, within the bound.
A program may use at most 128 MiB of HBM per device.

v0:
```python
import jax
import jax.numpy as jnp
from jax import lax
from jax.sharding import PartitionSpec as P

HDIM = 64
BLK = 256
BLK_DEV = 8
EPSILON = 1e-06
RATE_SCALE = 0.1


def norm_rows(values, gain_vector):
    widened = values.astype(jnp.float32)
    factor = lax.rsqrt(jnp.mean(widened * widened, axis=-1, keepdims=True) + EPSILON)
    return (widened * factor * gain_vector).astype(jnp.bfloat16)


def attend_pair(pieces):
    query_rows, key_rows, value_rows, token_ids = pieces
    token_count = query_rows.shape[0]
    heads_here = query_rows.shape[1] // HDIM
    q_heads = query_rows.reshape(token_count, heads_here, HDIM)
    k_heads = key_rows.reshape(token_count, heads_here, HDIM)
    v_heads = value_rows.reshape(token_count, heads_here, HDIM)
    scores = jnp.einsum(
        "qhe,khe->hqk", q_heads, k_heads, preferred_element_type=jnp.float32
    ) * HDIM ** (-0.5)
    allowed = token_ids[:, None] == token_ids[None, :]
    scores = jnp.where(allowed[None], scores, -1e30)
    top_score = jnp.max(scores, axis=-1, keepdims=True)
    exp_scores = jnp.exp(scores - top_score)
    weights = (exp_scores / jnp.sum(exp_scores, axis=-1, keepdims=True)).astype(jnp.bfloat16)
    mixed_heads = jnp.einsum("hqk,khe->qhe", weights, v_heads, preferred_element_type=jnp.float32)
    return mixed_heads.astype(jnp.bfloat16).reshape(token_count, heads_here * HDIM)


def encode_blocks(full_rows, block_ids, enc_gain, w_qkv):
    normed = norm_rows(full_rows, enc_gain)
    query_rows = jnp.dot(normed, w_qkv[0], preferred_element_type=jnp.float32).astype(jnp.bfloat16)
    key_rows = jnp.dot(normed, w_qkv[1], preferred_element_type=jnp.float32).astype(jnp.bfloat16)
    value_rows = jnp.dot(normed, w_qkv[2], preferred_element_type=jnp.float32).astype(jnp.bfloat16)
    columns = query_rows.shape[1]
    span = 2 * BLK
    pair_count = full_rows.shape[0] // span
    token_ids = jnp.repeat(block_ids, BLK, total_repeat_length=pair_count * span).reshape(
        pair_count, span
    )
    attended = lax.map(
        attend_pair,
        (
            query_rows.reshape(pair_count, span, columns),
            key_rows.reshape(pair_count, span, columns),
            value_rows.reshape(pair_count, span, columns),
            token_ids,
        ),
    )
    return attended.reshape(pair_count * span, columns)


def route_matrix(destinations, seq_count, room):
    slot_count = destinations.shape[0]
    target_seq = jnp.where(destinations >= 0, destinations // BLK_DEV, -1)
    position = jnp.arange(slot_count)
    earlier = position[None, :] < position[:, None]
    same_target = (target_seq[None, :] == target_seq[:, None]) & earlier
    ranking = jnp.sum(same_target.astype(jnp.int32), axis=1)
    bucket = jnp.where(destinations >= 0, target_seq * room + ranking, -1)
    return bucket[None, :] == jnp.arange(seq_count * room)[:, None]


def pack_rows(selection, payload):
    return jnp.dot(
        selection.astype(jnp.bfloat16), payload, preferred_element_type=jnp.float32
    ).astype(jnp.bfloat16)


def pack_index(selection, indices):
    return jnp.sum(jnp.where(selection, indices[None, :] + 1, 0), axis=1).astype(jnp.int32) - 1


def place_matrix(arrived, seq_index):
    local_block = arrived - seq_index * BLK_DEV
    return (local_block[None, :] == jnp.arange(BLK_DEV)[:, None]) & (arrived >= 0)[None, :]


def renorm(updated, initial):
    target_norm = jnp.sqrt(jnp.sum(initial * initial, axis=1, keepdims=True))
    return (
        updated
        * target_norm
        * lax.rsqrt(jnp.sum(updated * updated, axis=1, keepdims=True) + EPSILON)
    )


def on_device(
    patches,
    slot_image,
    slot_dest,
    enc_gain,
    w_qkv,
    w_out,
    fast_gain,
    w_fast,
    w_rate,
    fast_gate_up,
    fast_down,
):
    seq_count = lax.axis_size("seq")
    seq_index = lax.axis_index("seq")
    head_index = lax.axis_index("head")
    width = w_out.shape[0]
    slot_count = slot_dest.shape[0]
    room = 2 * ((BLK_DEV + seq_count - 1) // seq_count)
    patch_blocks = patches.reshape(slot_count, BLK, patches.shape[1])
    own_columns = lax.dynamic_slice_in_dim(patch_blocks, head_index * width, width, 2).reshape(
        slot_count, BLK * width
    )
    selection = route_matrix(slot_dest, seq_count, room)
    sent_dest = pack_index(selection, slot_dest)
    got_own, arrived, got_ids = (
        lax.all_to_all(
            pack_rows(selection, own_columns), "seq", split_axis=0, concat_axis=0, tiled=True
        ),
        lax.all_to_all(sent_dest, "seq", split_axis=0, concat_axis=0, tiled=True),
        lax.all_to_all(
            pack_index(selection, slot_image), "seq", split_axis=0, concat_axis=0, tiled=True
        ),
    )
    placing = place_matrix(arrived, seq_index)
    view_own = pack_rows(placing, got_own)
    view_ids = pack_index(placing, got_ids)
    whole_rows = lax.all_gather(view_own.reshape(BLK_DEV * BLK, width), "head", axis=1, tiled=True)
    view_attn = encode_blocks(whole_rows, view_ids, enc_gain, w_qkv)
    partial_value = jnp.dot(view_attn, w_out, preferred_element_type=jnp.float32)
    head_mixed = lax.psum_scatter(
        partial_value.astype(jnp.bfloat16), "head", scatter_dimension=1, tiled=True
    ).astype(jnp.float32)
    embedded = (head_mixed + view_own.reshape(BLK_DEV * BLK, width).astype(jnp.float32)).astype(
        jnp.bfloat16
    )
    full_embedded = lax.all_gather(embedded, "head", axis=1, tiled=True)
    normed_fast = norm_rows(full_embedded, fast_gain)
    fast_query = jnp.dot(normed_fast, w_fast[0], preferred_element_type=jnp.float32).astype(
        jnp.bfloat16
    )
    fast_key = jnp.dot(normed_fast, w_fast[1], preferred_element_type=jnp.float32).astype(
        jnp.bfloat16
    )
    fast_value = jnp.dot(normed_fast, w_fast[2], preferred_element_type=jnp.float32).astype(
        jnp.bfloat16
    )
    token_total = embedded.shape[0] * seq_count
    rates = (
        RATE_SCALE
        * jax.nn.softplus(jnp.dot(normed_fast, w_rate, preferred_element_type=jnp.float32))
        * token_total ** (-0.5)
    )
    gate_init = fast_gate_up[0, 0]
    up_init = fast_gate_up[0, 1]
    down_init = fast_down[0]
    gate_half = gate_init.astype(jnp.bfloat16)
    up_half = up_init.astype(jnp.bfloat16)
    down_half = down_init.astype(jnp.bfloat16)
    key_gate = jnp.dot(fast_key, gate_half, preferred_element_type=jnp.float32)
    key_up = jnp.dot(fast_key, up_half, preferred_element_type=jnp.float32)
    hidden_key = (jax.nn.silu(key_gate) * key_up).astype(jnp.bfloat16)
    out_grad = (-rates * fast_value.astype(jnp.float32)).astype(jnp.bfloat16)
    grad_down = jnp.einsum("th,tf->hf", hidden_key, out_grad, preferred_element_type=jnp.float32)
    hidden_grad = jnp.dot(out_grad, down_half.T, preferred_element_type=jnp.float32)
    sigmoid_gate = jax.nn.sigmoid(key_gate)
    gate_grad = (
        hidden_grad * key_up * sigmoid_gate * (1.0 + key_gate * (1.0 - sigmoid_gate))
    ).astype(jnp.bfloat16)
    up_grad = (hidden_grad * jax.nn.silu(key_gate)).astype(jnp.bfloat16)
    grad_gate = jnp.einsum("tf,th->fh", fast_key, gate_grad, preferred_element_type=jnp.float32)
    grad_up = jnp.einsum("tf,th->fh", fast_key, up_grad, preferred_element_type=jnp.float32)
    grad_gate, grad_up, grad_down = (
        lax.psum(grad_gate.astype(jnp.bfloat16), "seq").astype(jnp.float32),
        lax.psum(grad_up.astype(jnp.bfloat16), "seq").astype(jnp.float32),
        lax.psum(grad_down.astype(jnp.bfloat16), "seq").astype(jnp.float32),
    )
    new_gate = renorm(gate_init - grad_gate, gate_init)
    new_up = renorm(up_init - grad_up, up_init)
    new_down = renorm(down_init - grad_down, down_init)
    applied_gate = new_gate.astype(jnp.bfloat16)
    applied_up = new_up.astype(jnp.bfloat16)
    applied_down = new_down.astype(jnp.bfloat16)
    query_gate = jnp.dot(fast_query, applied_gate, preferred_element_type=jnp.float32)
    query_up = jnp.dot(fast_query, applied_up, preferred_element_type=jnp.float32)
    query_hidden = (jax.nn.silu(query_gate) * query_up).astype(jnp.bfloat16)
    fast_out = jnp.dot(query_hidden, applied_down, preferred_element_type=jnp.float32)
    return (embedded.astype(jnp.float32) + fast_out).astype(jnp.bfloat16)


def solution(mesh):
    in_specs = (
        P("seq", None),
        P("seq"),
        P("seq"),
        P(),
        P(None, None, "head"),
        P("head", None),
        P(),
        P(None, None, "head"),
        P(None, "head"),
        P("head", None, None, None),
        P("head", None, None),
    )
    out_specs = P("seq", "head")
    return jax.shard_map(
        on_device, mesh=mesh, in_specs=in_specs, out_specs=out_specs, check_vma=False
    )
```

profile of v0, /device:TPU:0, one launch (start us, length us, event | category | flops | bytes accessed | tf_op | source)
XLA Modules:
  0.0 311.4 jit_solution(212847610619158784)
XLA Ops:
  6.5 0.7 broadcast_add_fusion.3
  7.2 0.7 broadcast_add_fusion.4
  8.1 0.7 compare_select_fusion.4
  8.9 0.7 sub.54
  9.6 7.3 %all-to-all-start = ((s32[8,2,1]{1,2,0:T(1,128)}), s32[8,2,1]{1,2,0:T(1,128)S(1)}, u32[]{:S(2)}, u32[]{:S(2)}) async-start(s32[8,2,1]{1,2,0:T(1,128)} %bitcast.6), calls=%async_computation | async-start | bytes 8192 | tf_op jit(solution)/shard_map/all_to_all | solution.py:125
  16.8 2.9 constant_dynamic-slice_fusion.4
  19.8 3.2 %reshape.274 = bf16[16,49152]{1,0:T(8,128)(2,1)} reshape(bf16[16,256,192]{2,1,0:T(8,128)(2,1)S(1)} %constant_dynamic-slice_fusion.4) | data formatting | bytes 3145728 | tf_op jit(solution)/shard_map/reshape | solution.py:116
  23.0 2.0 convolution_convert_fusion
  24.9 1.9 all_to_all.17
  26.9 6.0 %all-to-all-start.1 = ((bf16[8,2,49152]{2,1,0:T(2,128)(2,1)}), bf16[8,2,49152]{2,1,0:T(2,128)(2,1)S(1)}, u32[]{:S(2)}, u32[]{:S(2)}) async-start(bf16[8,2,49152]{2,1,0:T(2,128)(2,1)} %all_to_all.17), calls=%async_computation.1 | async-start | bytes 3145728 | tf_op jit(solution)/shard_map/all_to_all | solution.py:122
  33.1 36.2 %all-to-all-done.1 = bf16[8,2,49152]{2,1,0:T(2,128)(2,1)S(1)} async-done(((bf16[8,2,49152]{2,1,0:T(2,128)(2,1)}), bf16[8,2,49152]{2,1,0:T(2,128)(2,1)S(1)}, u32[]{:S(2)}, u32[]{:S(2)}) %all-to-all-start.1) | async-done | bytes 1572896 | tf_op jit(solution)/shard_map/all_to_all | solution.py:122
  69.3 0.6 all_to_all.19
  70.0 1.2 convolution_convert_fusion.1
  71.3 2.3 reshape.275
  73.6 1.2 copy.34
  74.9 0.7 sub.59
  75.5 3.6 %all-to-all-start.2 = ((s32[8,2,1]{1,2,0:T(1,128)}), s32[8,2,1]{1,2,0:T(1,128)S(1)}, u32[]{:S(2)}, u32[]{:S(2)}) async-start(s32[8,2,1]{1,2,0:T(1,128)} %bitcast.9), calls=%async_computation.2 | async-start | bytes 8192 | tf_op jit(solution)/shard_map/all_to_all | solution.py:126
  79.2 0.2 reduce-scatter.2.cloned.1.call-start
  79.4 6.3 %all-to-all-done.2 = s32[8,2,1]{1,2,0:T(1,128)S(1)} async-done(((s32[8,2,1]{1,2,0:T(1,128)}), s32[8,2,1]{1,2,0:T(1,128)S(1)}, u32[]{:S(2)}, u32[]{:S(2)}) %all-to-all-start.2) | async-done | bytes 96 | tf_op jit(solution)/shard_map/all_to_all | solution.py:126
  85.9 0.7 fusion.74
  86.6 5.0 %select_select_fusion = s32[2048]{0:T(1024)S(1)} fusion(pred[2048]{0:T(1024)(128)(4,1)S(1)} %copy-done.21, pred[2048]{0:T(1024)(128)(4,1)S(1)} %copy-done.20, pred[2048]{0:T(1024)(128)(4,1)S(1)} %copy-done.19, pred[2048]{0:T(1024)(128)(4,1)S(1)} %copy-done.18, pred[2048]{0:T(1024)(128)(4,1)S(1)} %copy-done.17, pred[2048]{0:T(1024)(128)(4,1)S(1)} %copy-done.16, ...), kind=kLoop, calls=%fused_computation.103 | loop fusion | flops 14336 | bytes 22560 | tf_op jit(solution)/shard_map/jit(_take)/gather | solution.py:46
  91.6 10.7 %all-gather.3.cloned.1.call-done = bf16[2048,768]{0,1:T(8,128)(2,1)} async-done(((bf16[2048,192]{0,1:T(8,128)(2,1)}), bf16[2048,768]{0,1:T(8,128)(2,1)}) %all-gather.3.cloned.1.call-update) | async-done | bytes 3145744 | tf_op jit(solution)/shard_map/all_gather | solution.py:133
  102.3 2.7 fusion.11
  105.1 1.1 convolution_convert_fusion.7
  106.3 1.1 convolution_convert_fusion.6
  107.5 1.1 convolution_convert_fusion.8
  108.6 25.0 %while.11 = (s32[]{:T(128)}, bf16[4,512,192]{1,2,0:T(8,128)(2,1)}, bf16[4,512,192]{1,2,0:T(8,128)(2,1)S(1)}, s32[4,512]{1,0:T(4,128)S(1)}, bf16[4,512,192]{1,2,0...) while((s32[]{:T(128)}, bf16[4,512,192]{1,2,0:T(8,128)(2,1)}, ...), condition=%wide.region_8.9_spmd, body=%wide.region_5.8_spmd.sunk | while | flops 206406144 | bytes 9193573 | solution.py:49
  109.0 3.0 fusion.111
  111.9 2.3 fusion.112
  114.2 0.7 constant_dynamic-update-slice_fusion.2
  115.2 3.0 fusion.111
  118.2 2.3 fusion.112
  120.5 0.7 constant_dynamic-update-slice_fusion.2
  121.4 3.0 fusion.111
  124.4 2.3 fusion.112
  126.7 0.7 constant_dynamic-update-slice_fusion.2
  127.7 3.0 fusion.111
  130.6 2.3 fusion.112
  132.9 0.7 constant_dynamic-update-slice_fusion.2
  133.6 1.2 copy.45
  134.9 2.7 convolution_convert_fusion.2
  137.6 38.0 %reduce-scatter.2.cloned.1.call-done = bf16[2048,192]{0,1:T(8,128)(2,1)} async-done(((bf16[2048,768]{0,1:T(8,128)(2,1)}), bf16[2048,192]{0,1:T(8,128)(2,1)}) %reduce-scatter.2.cloned.1.call-update) | async-done | bytes 786448 | tf_op jit(solution)/shard_map/reduce_scatter | solution.py:136
  175.6 2.3 add_convert_fusion
  177.9 0.3 all-reduce.3.cloned.1.call-start
  178.2 28.4 %all-gather.5.cloned.1.call-done = bf16[2048,768]{0,1:T(8,128)(2,1)} async-done(((bf16[2048,192]{0,1:T(8,128)(2,1)}), bf16[2048,768]{0,1:T(8,128)(2,1)}) %all-gather.5.cloned.1.call-update) | async-done | bytes 3145744 | tf_op jit(solution)/shard_map/all_gather | solution.py:142
  206.6 2.7 fusion.14
  209.4 0.7 fusion.16
  210.2 0.4 copy-done.10
  210.6 0.8 convolution_convert_fusion.4
  211.4 0.2 copy-done.3
  211.7 0.8 fusion.46
  212.4 0.8 fusion.48
  213.2 0.5 fusion.78
  213.7 0.8 fusion.21
  214.7 0.7 fusion.75
  215.4 1.8 fusion.25
  217.3 2.1 fusion.27
  219.4 1.8 fusion.26
  221.2 2.6 convolution_convert_fusion.5
  223.8 70.4 %all-reduce.3.cloned.1.call-done = (bf16[192,384]{1,0:T(8,128)(2,1)}, bf16[192,384]{1,0:T(8,128)(2,1)}, bf16[384,192]{0,1:T(8,128)(2,1)}) async-done(((bf16[192,384]{1,0:T(8,128)(2,1)}, bf16[192,384]{1,0:T(8,128)(2,1)}, bf16[384,192]{0,1:T(8,128)(2,1)}), (bf16[192,384]{1,0:T(8,128)(2,1)}, bf16[192,384]{1,0:T(8,128)(2,1)}, bf16[384,192]{0,1:T(8,128)(2,1)})) %all-reduce.3.cloned.1.call-update) | async-done | bytes 442384 | tf_op jit(solution)/shard_map/psum | solution.py:179
  294.2 1.4 fusion.30
  295.7 1.1 fusion.31
  296.8 3.8 %fusion.45 = f32[2048,384]{1,0:T(8,128)} fusion(bf16[2048,192]{0,1:T(8,128)(2,1)} %convolution_convert_fusion.5, bf16[192,384]{1,0:T(8,128)(2,1)} %get-tuple-element.94, f32[1,2,192,384]{3,2,1,0:T(8,128)} %param.24, f32[192]{0:T(256)S(1)} %add_rsqrt_fusion.4, f32[192]{0:T(256)S(1)} %sqrt.24), kind=kOutput, calls=%fused_computation.89 | convolution fusion | flops 302358528 | bytes 4376064 | tf_op jit(solution)/shard_map/dot_general | solution.py:189
  300.6 4.3 %fusion.18 = bf16[2048,192]{0,1:T(8,128)(2,1)} fusion(bf16[2048,192]{0,1:T(8,128)(2,1)S(1)} %copy-done.6, f32[2048,384]{1,0:T(8,128)} %fusion.45, bf16[2048,192]{0,1:T(8,128)(2,1)S(1)} %copy-done.7, bf16[192,384]{1,0:T(8,128)(2,1)S(1)} %copy-done.11, f32[1,2,192,384]{3,2,1,0:T(8,128)S(1)} %copy-done.4, bf16[384,192]{0,1:T(8,128)(2,1)S(1)} %copy-done.12, ...), kind=kOutput, calls=%fused_computation.39 | convolution fusion | flops 610615296 | bytes 6395904 | tf_op jit(solution)/shard_map/dot_general | solution.py:192
  (94 shorter events, 2.7 us)
Async XLA Ops:
  6.5 128.3 %copy-start = (bf16[192,768]{1,0:T(8,128)(2,1)S(1)}, bf16[192,768]{1,0:T(8,128)(2,1)}, u32[]{:S(2)}) copy-start(bf16[192,768]{1,0:T(8,128)(2,1)} %param.20) | copy-start | bytes 884740
  9.6 17.3 %all-to-all-start = ((s32[8,2,1]{1,2,0:T(1,128)}), s32[8,2,1]{1,2,0:T(1,128)S(1)}, u32[]{:S(2)}, u32[]{:S(2)}) async-start(s32[8,2,1]{1,2,0:T(1,128)} %bitcast.6), calls=%async_computation | async-start | bytes 8192 | tf_op jit(solution)/shard_map/all_to_all | solution.py:125
  26.9 42.4 %all-to-all-start.1 = ((bf16[8,2,49152]{2,1,0:T(2,128)(2,1)}), bf16[8,2,49152]{2,1,0:T(2,128)(2,1)S(1)}, u32[]{:S(2)}, u32[]{:S(2)}) async-start(bf16[8,2,49152]{2,1,0:T(2,128)(2,1)} %all_to_all.17), calls=%async_computation.1 | async-start | bytes 3145728 | tf_op jit(solution)/shard_map/all_to_all | solution.py:122
  32.9 69.4 %all-gather.3.cloned.1.call-start = ((), (), s32[]{:S(2)}) async-start(), calls=%async_computation.4 | async-start | bytes 3932160 | tf_op jit(solution)/shard_map/all_gather | solution.py:133
  69.9 16.6 %copy-start.15 = (pred[2048]{0:T(1024)(128)(4,1)S(1)}, pred[2048]{0:T(1024)(128)(4,1)}, u32[]{:S(2)}) copy-start(pred[2048]{0:T(1024)(128)(4,1)} %constant.200) | copy-start | bytes 6148
  70.0 16.6 %copy-start.16 = (pred[2048]{0:T(1024)(128)(4,1)S(1)}, pred[2048]{0:T(1024)(128)(4,1)}, u32[]{:S(2)}) copy-start(pred[2048]{0:T(1024)(128)(4,1)} %constant.199) | copy-start | bytes 6148
  70.0 16.6 %copy-start.17 = (pred[2048]{0:T(1024)(128)(4,1)S(1)}, pred[2048]{0:T(1024)(128)(4,1)}, u32[]{:S(2)}) copy-start(pred[2048]{0:T(1024)(128)(4,1)} %constant.198) | copy-start | bytes 6148
  70.0 16.6 %copy-start.18 = (pred[2048]{0:T(1024)(128)(4,1)S(1)}, pred[2048]{0:T(1024)(128)(4,1)}, u32[]{:S(2)}) copy-start(pred[2048]{0:T(1024)(128)(4,1)} %constant.197) | copy-start | bytes 6148
  70.0 16.6 %copy-start.19 = (pred[2048]{0:T(1024)(128)(4,1)S(1)}, pred[2048]{0:T(1024)(128)(4,1)}, u32[]{:S(2)}) copy-start(pred[2048]{0:T(1024)(128)(4,1)} %constant.196) | copy-start | bytes 6148
  70.0 16.6 %copy-start.20 = (pred[2048]{0:T(1024)(128)(4,1)S(1)}, pred[2048]{0:T(1024)(128)(4,1)}, u32[]{:S(2)}) copy-start(pred[2048]{0:T(1024)(128)(4,1)} %constant.195) | copy-start | bytes 6148
  70.0 16.6 %copy-start.21 = (pred[2048]{0:T(1024)(128)(4,1)S(1)}, pred[2048]{0:T(1024)(128)(4,1)}, u32[]{:S(2)}) copy-start(pred[2048]{0:T(1024)(128)(4,1)} %constant.194) | copy-start | bytes 6148
  73.6 31.4 %copy-start.22 = (bf16[3,768,192]{1,2,0:T(8,128)(2,1)S(1)}, bf16[3,768,192]{1,2,0:T(8,128)(2,1)}, u32[]{:S(2)}) copy-start(bf16[3,768,192]{1,2,0:T(8,128)(2,1)} %param.19) | copy-start | bytes 2654212
  73.6 31.4 %copy-start.23 = (f32[768]{0:T(1024)S(1)}, f32[768]{0:T(1024)}, u32[]{:S(2)}) copy-start(f32[768]{0:T(1024)} %param.18) | copy-start | bytes 9220
  75.5 10.1 %all-to-all-start.2 = ((s32[8,2,1]{1,2,0:T(1,128)}), s32[8,2,1]{1,2,0:T(1,128)S(1)}, u32[]{:S(2)}, u32[]{:S(2)}) async-start(s32[8,2,1]{1,2,0:T(1,128)} %bitcast.9), calls=%async_computation.2 | async-start | bytes 8192 | tf_op jit(solution)/shard_map/all_to_all | solution.py:126
  79.2 96.4 %reduce-scatter.2.cloned.1.call-start = ((), (), s32[]{:S(2)}) async-start(), calls=%async_computation.5 | async-start | bytes 3932160 | tf_op jit(solution)/shard_map/reduce_scatter | solution.py:136
  102.3 2.8 copy-start.5
  137.6 38.1 %copy-start.2 = (bf16[2048,192]{0,1:T(8,128)(2,1)S(1)}, bf16[2048,192]{0,1:T(8,128)(2,1)}, u32[]{:S(2)}) copy-start(bf16[2048,192]{0,1:T(8,128)(2,1)} %copy.34) | copy-start | bytes 2359300
  137.6 71.7 %copy-start.13 = (f32[768]{0:T(1024)S(1)}, f32[768]{0:T(1024)}, u32[]{:S(2)}) copy-start(f32[768]{0:T(1024)} %param.21) | copy-start | bytes 9220
  137.6 69.0 %all-gather.5.cloned.1.call-start = ((), (), s32[]{:S(2)}) async-start(), calls=%async_computation.6 | async-start | bytes 3932160 | tf_op jit(solution)/shard_map/all_gather | solution.py:142
  177.9 116.3 %all-reduce.3.cloned.1.call-start = ((), (), s32[]{:S(2)}) async-start(), calls=%async_computation.7 | async-start | bytes 884736 | tf_op jit(solution)/shard_map/psum | solution.py:179
  206.6 2.8 copy-start.1
  209.4 1.2 copy-start.10
  210.6 1.1 copy-start.3
  212.4 0.8 copy-start.14
  213.7 1.0 copy-start.8
  223.8 76.7 %copy-start.4 = (f32[1,2,192,384]{3,2,1,0:T(8,128)S(1)}, f32[1,2,192,384]{3,2,1,0:T(8,128)}, u32[]{:S(2)}) copy-start(f32[1,2,192,384]{3,2,1,0:T(8,128)} %param.24) | copy-start | bytes 1769476
  223.8 76.7 %copy-start.6 = (bf16[2048,192]{0,1:T(8,128)(2,1)S(1)}, bf16[2048,192]{0,1:T(8,128)(2,1)}, u32[]{:S(2)}) copy-start(bf16[2048,192]{0,1:T(8,128)(2,1)} %add_convert_fusion) | copy-start | bytes 2359300
  223.8 76.7 %copy-start.7 = (bf16[2048,192]{0,1:T(8,128)(2,1)S(1)}, bf16[2048,192]{0,1:T(8,128)(2,1)}, u32[]{:S(2)}) copy-start(bf16[2048,192]{0,1:T(8,128)(2,1)} %convolution_convert_fusion.5) | copy-start | bytes 2359300
  223.8 76.7 %copy-start.9 = (f32[1,384,192]{1,2,0:T(8,128)S(1)}, f32[1,384,192]{1,2,0:T(8,128)}, u32[]{:S(2)}) copy-start(f32[1,384,192]{1,2,0:T(8,128)} %param.25) | copy-start | bytes 884740
  294.2 6.3 %copy-start.11 = (bf16[192,384]{1,0:T(8,128)(2,1)S(1)}, bf16[192,384]{1,0:T(8,128)(2,1)}, u32[]{:S(2)}) copy-start(bf16[192,384]{1,0:T(8,128)(2,1)} %get-tuple-element.95) | copy-start | bytes 442372
  294.2 6.3 %copy-start.12 = (bf16[384,192]{0,1:T(8,128)(2,1)S(1)}, bf16[384,192]{0,1:T(8,128)(2,1)}, u32[]{:S(2)}) copy-start(bf16[384,192]{0,1:T(8,128)(2,1)} %get-tuple-element.96) | copy-start | bytes 442372
Sparse Core Ops, SparseCore 0:
  75.0 27.2 all-gather.2
  137.7 37.8 reduce-scatter.1
  178.1 28.4 all-gather.4
  221.3 72.8 all-reduce.2
where the time goes:
time: 312 us; the launch traced here: 311 us
  waiting for transfers between devices  190 us (61%)
  matrix products  50.9 us (16%)
  local copies, waits for them, and re-layouts  20.1 us (6%)
  other arithmetic  19.3 us (6%)
  starting transfers between devices  17.5 us (6%)
  between operations  13.5 us (4%)
    psum x1, waiting for transfers between devices, on_device(): lax.psum(grad_gate.astype(jnp.bfloat16), 'seq').astype(jnp.float32)  70.4 us
    reduce_scatter x1, waiting for transfers between devices, on_device(): lax.psum_scatter(partial_value.astype(jnp.bfloat16), 'head', scatter_dime...  38 us
    all_to_all x1, waiting for transfers between devices, on_device(): lax.all_to_all(pack_rows(selection, own_columns), 'seq', split_axis=0, co...  36.2 us
    all_gather x1, waiting for transfers between devices, on_device(): full_embedded = lax.all_gather(embedded, 'head', axis=1, tiled=True)  28.4 us
    sub x4, matrix products, attend_pair(): exp_scores = jnp.exp(scores - top_score)  11.9 us
    all_gather x1, waiting for transfers between devices, on_device(): lax.all_gather(view_own.reshape(BLK_DEV * BLK, width), 'head', axis=1, ti...  10.7 us
    dot_general x4, matrix products, attend_pair(): jnp.einsum('hqk,khe->qhe', weights, v_heads, preferred_element_type=jnp.f...  9.15 us
    all_to_all x1, starting transfers between devices, on_device(): lax.all_to_all(sent_dest, 'seq', split_axis=0, concat_axis=0, tiled=True)  7.28 us
  transfers between devices with their start and end apart: 7, of which 6 were waited for; matrix products, arithmetic and copies ran while one was open for 6% of the time, Pallas kernels for 0%

commit v1 on v0

--- a/solution.py
+++ b/solution.py
@@ -139,7 +139,7 @@
     embedded = (head_mixed + view_own.reshape(BLK_DEV * BLK, width).astype(jnp.float32)).astype(
         jnp.bfloat16
     )
-    full_embedded = lax.all_gather(embedded, "head", axis=1, tiled=True)
+    full_embedded = jnp.concatenate(lax.all_gather(embedded, "head"), axis=1)
     normed_fast = norm_rows(full_embedded, fast_gain)
     fast_query = jnp.dot(normed_fast, w_fast[0], preferred_element_type=jnp.float32).astype(
         jnp.bfloat16

time: 312 us -> 323 us (1.035)
  local copies, waits for them, and re-layouts: 20.1 us -> 28.3 us
    convert_element_type x0 -> x1, local copies, waits for them, and re-layouts: none -> 8.34 us  [norm_rows(): widened = values.astype(jnp.float32)]
  transfers between devices with their start and end apart: 7 -> 7, of which waited for: 6 -> 6; matrix products, arithmetic and copies ran while one was open for 6% -> 5% of each run, Pallas kernels for 0% -> 0%
where the time goes in v1:
time: 323 us; the launch traced here: 322 us
  waiting for transfers between devices  190 us (59%)
  matrix products  51 us (16%)
  local copies, waits for them, and re-layouts  28.3 us (9%)
  other arithmetic  21.3 us (7%)
  starting transfers between devices  17.3 us (5%)
  between operations  13.6 us (4%)
    psum x1, waiting for transfers between devices, on_device(): lax.psum(grad_gate.astype(jnp.bfloat16), 'seq').astype(jnp.float32)  70.4 us
    reduce_scatter x1, waiting for transfers between devices, on_device(): lax.psum_scatter(partial_value.astype(jnp.bfloat16), 'head', scatter_dime...  38 us
    all_to_all x1, waiting for transfers between devices, on_device(): lax.all_to_all(pack_rows(selection, own_columns), 'seq', split_axis=0, co...  36.2 us
    all_gather x1, waiting for transfers between devices, on_device(): full_embedded = jnp.concatenate(lax.all_gather(embedded, 'head'), axis=1)  28.5 us
    sub x4, matrix products, attend_pair(): exp_scores = jnp.exp(scores - top_score)  11.9 us
    all_gather x1, waiting for transfers between devices, on_device(): lax.all_gather(view_own.reshape(BLK_DEV * BLK, width), 'head', axis=1, ti...  10.7 us
    dot_general x4, matrix products, attend_pair(): jnp.einsum('hqk,khe->qhe', weights, v_heads, preferred_element_type=jnp.f...  9.15 us
    convert_element_type x1, local copies, waits for them, and re-layouts, norm_rows(): widened = values.astype(jnp.float32)  8.34 us
  transfers between devices with their start and end apart: 7, of which 6 were waited for; matrix products, arithmetic and copies ran while one was open for 5% of the time, Pallas kernels for 0%

profile of v1, /device:TPU:0, one launch (start us, length us, event | category | flops | bytes accessed | tf_op | source)
XLA Modules:
  0.0 321.6 jit_solution(14058343512872320088)
XLA Ops:
  6.5 0.7 broadcast_add_fusion.3
  7.2 0.7 broadcast_add_fusion.4
  8.1 0.7 compare_select_fusion.4
  8.9 0.7 sub.54
  9.6 7.3 %all-to-all-start = ((s32[8,2,1]{1,2,0:T(1,128)}), s32[8,2,1]{1,2,0:T(1,128)S(1)}, u32[]{:S(2)}, u32[]{:S(2)}) async-start(s32[8,2,1]{1,2,0:T(1,128)} %bitcast.6), calls=%async_computation | async-start | bytes 8192 | tf_op jit(solution)/shard_map/all_to_all | solution.py:125
  16.8 2.9 constant_dynamic-slice_fusion.4
  19.8 3.2 reshape.317
  23.0 2.0 convolution_convert_fusion
  24.9 1.9 all_to_all.17
  26.9 6.0 %all-to-all-start.1 = ((bf16[8,2,49152]{2,1,0:T(2,128)(2,1)}), bf16[8,2,49152]{2,1,0:T(2,128)(2,1)S(1)}, u32[]{:S(2)}, u32[]{:S(2)}) async-start(bf16[8,2,49152]{2,1,0:T(2,128)(2,1)} %all_to_all.17), calls=%async_computation.1 | async-start | bytes 3145728 | tf_op jit(solution)/shard_map/all_to_all | solution.py:122
  33.1 36.2 %all-to-all-done.1 = bf16[8,2,49152]{2,1,0:T(2,128)(2,1)S(1)} async-done(((bf16[8,2,49152]{2,1,0:T(2,128)(2,1)}), bf16[8,2,49152]{2,1,0:T(2,128)(2,1)S(1)}, u32[]{:S(2)}, u32[]{:S(2)}) %all-to-all-start.1) | async-done | bytes 1572896 | tf_op jit(solution)/shard_map/all_to_all | solution.py:122
  69.3 0.6 all_to_all.19
  70.0 1.2 convolution_convert_fusion.1
  71.3 2.3 reshape.318
  73.6 1.2 copy.36
  74.9 0.7 sub.59
  75.5 3.6 %all-to-all-start.2 = ((s32[8,2,1]{1,2,0:T(1,128)}), s32[8,2,1]{1,2,0:T(1,128)S(1)}, u32[]{:S(2)}, u32[]{:S(2)}) async-start(s32[8,2,1]{1,2,0:T(1,128)} %bitcast.9), calls=%async_computation.2 | async-start | bytes 8192 | tf_op jit(solution)/shard_map/all_to_all | solution.py:126
  79.2 0.2 reduce-scatter.2.cloned.1.call-start
  79.4 6.3 %all-to-all-done.2 = s32[8,2,1]{1,2,0:T(1,128)S(1)} async-done(((s32[8,2,1]{1,2,0:T(1,128)}), s32[8,2,1]{1,2,0:T(1,128)S(1)}, u32[]{:S(2)}, u32[]{:S(2)}) %all-to-all-start.2) | async-done | bytes 96 | tf_op jit(solution)/shard_map/all_to_all | solution.py:126
  85.9 0.7 fusion.73
  86.6 5.0 %select_select_fusion = s32[2048]{0:T(1024)S(1)} fusion(pred[2048]{0:T(1024)(128)(4,1)S(1)} %copy-done.22, pred[2048]{0:T(1024)(128)(4,1)S(1)} %copy-done.21, pred[2048]{0:T(1024)(128)(4,1)S(1)} %copy-done.20, pred[2048]{0:T(1024)(128)(4,1)S(1)} %copy-done.19, pred[2048]{0:T(1024)(128)(4,1)S(1)} %copy-done.18, pred[2048]{0:T(1024)(128)(4,1)S(1)} %copy-done.17, ...), kind=kLoop, calls=%fused_computation.102 | loop fusion | flops 14336 | bytes 22560 | tf_op jit(solution)/shard_map/jit(_take)/gather | solution.py:46
  91.6 10.7 %all-gather.4.cloned.1.call-done = bf16[2048,768]{0,1:T(8,128)(2,1)} async-done(((bf16[2048,192]{0,1:T(8,128)(2,1)}), bf16[2048,768]{0,1:T(8,128)(2,1)}) %all-gather.4.cloned.1.call-update) | async-done | bytes 3145744 | tf_op jit(solution)/shard_map/all_gather | solution.py:133
  102.3 2.7 fusion.11
  105.1 1.1 convolution_convert_fusion.7
  106.3 1.1 convolution_convert_fusion.6
  107.5 1.1 convolution_convert_fusion.8
  108.6 25.0 %while.11 = (s32[]{:T(128)}, bf16[4,512,192]{1,2,0:T(8,128)(2,1)}, bf16[4,512,192]{1,2,0:T(8,128)(2,1)S(1)}, s32[4,512]{1,0:T(4,128)S(1)}, bf16[4,512,192]{1,2,0...) while((s32[]{:T(128)}, bf16[4,512,192]{1,2,0:T(8,128)(2,1)}, ...), condition=%wide.region_8.9_spmd, body=%wide.region_5.8_spmd.sunk | while | flops 206406144 | bytes 9193573 | solution.py:49
  109.0 3.0 fusion.110
  111.9 2.3 fusion.111
  114.2 0.7 constant_dynamic-update-slice_fusion.2
  115.2 3.0 fusion.110
  118.2 2.3 fusion.111
  120.5 0.7 constant_dynamic-update-slice_fusion.2
  121.4 3.0 fusion.110
  124.4 2.3 fusion.111
  126.7 0.7 constant_dynamic-update-slice_fusion.2
  127.7 3.0 fusion.110
  130.6 2.3 fusion.111
  132.9 0.7 constant_dynamic-update-slice_fusion.2
  133.6 1.2 copy.49
  134.9 2.7 convolution_convert_fusion.2
  137.6 38.0 %reduce-scatter.2.cloned.1.call-done = bf16[2048,192]{0,1:T(8,128)(2,1)} async-done(((bf16[2048,768]{0,1:T(8,128)(2,1)}), bf16[2048,192]{0,1:T(8,128)(2,1)}) %reduce-scatter.2.cloned.1.call-update) | async-done | bytes 786448 | tf_op jit(solution)/shard_map/reduce_scatter | solution.py:136
  175.6 2.3 add_convert_fusion
  178.1 28.5 %all-gather.6.cloned.1.call-done = bf16[8192,192]{0,1:T(8,128)(2,1)} async-done(((bf16[2048,192]{0,1:T(8,128)(2,1)}), bf16[8192,192]{0,1:T(8,128)(2,1)}) %all-gather.6.cloned.1.call-update) | async-done | bytes 3145744 | tf_op jit(solution)/shard_map/all_gather | solution.py:142
  206.6 8.3 %reshape.340 = f32[4,2048,192]{1,0,2:T(4,128)} reshape(bf16[8192,192]{0,1:T(8,128)(2,1)} %all-gather.6.cloned.1.call-done) | data formatting | bytes 9437184 | tf_op jit(solution)/shard_map/convert_element_type | solution.py:14
  214.9 4.2 %multiply_reduce_fusion = f32[2048]{0:T(1024)S(1)} fusion(f32[4,2048,192]{1,0,2:T(4,128)} %reshape.340), kind=kLoop, calls=%fused_computation.29 | loop fusion | flops 3143680 | bytes 6299648 | tf_op jit(solution)/shard_map/reduce_sum | solution.py:15
  219.2 0.7 convert_element_type.176
  219.9 0.6 fusion.15
  220.5 0.5 copy-done.11
  221.1 0.8 convolution_convert_fusion.4
  221.9 0.8 fusion.45
  222.7 0.8 fusion.47
  223.4 0.5 fusion.77
  224.0 0.8 fusion.20
  224.9 0.8 fusion.74
  225.7 1.8 fusion.24
  227.5 2.1 fusion.26
  229.6 1.8 fusion.25
  231.4 2.6 convolution_convert_fusion.5
  234.1 70.4 %all-reduce.3.cloned.1.call-done = (bf16[192,384]{1,0:T(8,128)(2,1)}, bf16[192,384]{1,0:T(8,128)(2,1)}, bf16[384,192]{0,1:T(8,128)(2,1)}) async-done(((bf16[192,384]{1,0:T(8,128)(2,1)}, bf16[192,384]{1,0:T(8,128)(2,1)}, bf16[384,192]{0,1:T(8,128)(2,1)}), (bf16[192,384]{1,0:T(8,128)(2,1)}, bf16[192,384]{1,0:T(8,128)(2,1)}, bf16[384,192]{0,1:T(8,128)(2,1)})) %all-reduce.3.cloned.1.call-update) | async-done | bytes 442384 | tf_op jit(solution)/shard_map/psum | solution.py:179
  304.5 1.4 fusion.29
  305.9 1.0 fusion.30
  306.9 3.8 %fusion.44 = f32[2048,384]{1,0:T(8,128)} fusion(bf16[2048,192]{0,1:T(8,128)(2,1)} %convolution_convert_fusion.5, bf16[192,384]{1,0:T(8,128)(2,1)} %get-tuple-element.94, f32[1,2,192,384]{3,2,1,0:T(8,128)} %param.24, f32[192]{0:T(256)S(1)} %add_rsqrt_fusion.4, f32[192]{0:T(256)S(1)} %sqrt.24), kind=kOutput, calls=%fused_computation.88 | convolution fusion | flops 302358528 | bytes 4376064 | tf_op jit(solution)/shard_map/dot_general | solution.py:189
  310.7 4.3 %fusion.17 = bf16[2048,192]{0,1:T(8,128)(2,1)} fusion(bf16[2048,192]{0,1:T(8,128)(2,1)S(1)} %copy-done.7, f32[2048,384]{1,0:T(8,128)} %fusion.44, bf16[2048,192]{0,1:T(8,128)(2,1)S(1)} %copy-done.8, bf16[192,384]{1,0:T(8,128)(2,1)S(1)} %copy-done.12, f32[1,2,192,384]{3,2,1,0:T(8,128)S(1)} %copy-done.5, bf16[384,192]{0,1:T(8,128)(2,1)S(1)} %copy-done.13, ...), kind=kOutput, calls=%fused_computation.38 | convolution fusion | flops 610615296 | bytes 6395904 | tf_op jit(solution)/shard_map/dot_general | solution.py:192
  (99 shorter events, 2.7 us)
Async XLA Ops:
  6.5 128.3 %copy-start = (bf16[192,768]{1,0:T(8,128)(2,1)S(1)}, bf16[192,768]{1,0:T(8,128)(2,1)}, u32[]{:S(2)}) copy-start(bf16[192,768]{1,0:T(8,128)(2,1)} %param.20) | copy-start | bytes 884740
  9.6 17.3 %all-to-all-start = ((s32[8,2,1]{1,2,0:T(1,128)}), s32[8,2,1]{1,2,0:T(1,128)S(1)}, u32[]{:S(2)}, u32[]{:S(2)}) async-start(s32[8,2,1]{1,2,0:T(1,128)} %bitcast.6), calls=%async_computation | async-start | bytes 8192 | tf_op jit(solution)/shard_map/all_to_all | solution.py:125
  26.9 42.4 %all-to-all-start.1 = ((bf16[8,2,49152]{2,1,0:T(2,128)(2,1)}), bf16[8,2,49152]{2,1,0:T(2,128)(2,1)S(1)}, u32[]{:S(2)}, u32[]{:S(2)}) async-start(bf16[8,2,49152]{2,1,0:T(2,128)(2,1)} %all_to_all.17), calls=%async_computation.1 | async-start | bytes 3145728 | tf_op jit(solution)/shard_map/all_to_all | solution.py:122
  32.9 69.4 %all-gather.4.cloned.1.call-start = ((), (), s32[]{:S(2)}) async-start(), calls=%async_computation.4 | async-start | bytes 3932160 | tf_op jit(solution)/shard_map/all_gather | solution.py:133
  69.9 16.6 %copy-start.16 = (pred[2048]{0:T(1024)(128)(4,1)S(1)}, pred[2048]{0:T(1024)(128)(4,1)}, u32[]{:S(2)}) copy-start(pred[2048]{0:T(1024)(128)(4,1)} %constant.200) | copy-start | bytes 6148
  70.0 16.6 %copy-start.17 = (pred[2048]{0:T(1024)(128)(4,1)S(1)}, pred[2048]{0:T(1024)(128)(4,1)}, u32[]{:S(2)}) copy-start(pred[2048]{0:T(1024)(128)(4,1)} %constant.199) | copy-start | bytes 6148
  70.0 16.6 %copy-start.18 = (pred[2048]{0:T(1024)(128)(4,1)S(1)}, pred[2048]{0:T(1024)(128)(4,1)}, u32[]{:S(2)}) copy-start(pred[2048]{0:T(1024)(128)(4,1)} %constant.198) | copy-start | bytes 6148
  70.0 16.6 %copy-start.19 = (pred[2048]{0:T(1024)(128)(4,1)S(1)}, pred[2048]{0:T(1024)(128)(4,1)}, u32[]{:S(2)}) copy-start(pred[2048]{0:T(1024)(128)(4,1)} %constant.197) | copy-start | bytes 6148
  70.0 16.6 %copy-start.20 = (pred[2048]{0:T(1024)(128)(4,1)S(1)}, pred[2048]{0:T(1024)(128)(4,1)}, u32[]{:S(2)}) copy-start(pred[2048]{0:T(1024)(128)(4,1)} %constant.196) | copy-start | bytes 6148
  70.0 16.6 %copy-start.21 = (pred[2048]{0:T(1024)(128)(4,1)S(1)}, pred[2048]{0:T(1024)(128)(4,1)}, u32[]{:S(2)}) copy-start(pred[2048]{0:T(1024)(128)(4,1)} %constant.195) | copy-start | bytes 6148
  70.0 16.6 %copy-start.22 = (pred[2048]{0:T(1024)(128)(4,1)S(1)}, pred[2048]{0:T(1024)(128)(4,1)}, u32[]{:S(2)}) copy-start(pred[2048]{0:T(1024)(128)(4,1)} %constant.194) | copy-start | bytes 6148
  73.6 31.4 %copy-start.23 = (bf16[3,768,192]{1,2,0:T(8,128)(2,1)S(1)}, bf16[3,768,192]{1,2,0:T(8,128)(2,1)}, u32[]{:S(2)}) copy-start(bf16[3,768,192]{1,2,0:T(8,128)(2,1)} %param.19) | copy-start | bytes 2654212
  73.6 31.4 %copy-start.24 = (f32[768]{0:T(1024)S(1)}, f32[768]{0:T(1024)}, u32[]{:S(2)}) copy-start(f32[768]{0:T(1024)} %param.18) | copy-start | bytes 9220
  75.5 10.1 %all-to-all-start.2 = ((s32[8,2,1]{1,2,0:T(1,128)}), s32[8,2,1]{1,2,0:T(1,128)S(1)}, u32[]{:S(2)}, u32[]{:S(2)}) async-start(s32[8,2,1]{1,2,0:T(1,128)} %bitcast.9), calls=%async_computation.2 | async-start | bytes 8192 | tf_op jit(solution)/shard_map/all_to_all | solution.py:126
  79.2 96.4 %reduce-scatter.2.cloned.1.call-start = ((), (), s32[]{:S(2)}) async-start(), calls=%async_computation.5 | async-start | bytes 3932160 | tf_op jit(solution)/shard_map/reduce_scatter | solution.py:136
  102.3 2.8 copy-start.6
  137.6 38.1 %copy-start.3 = (bf16[2048,192]{0,1:T(8,128)(2,1)S(1)}, bf16[2048,192]{0,1:T(8,128)(2,1)}, u32[]{:S(2)}) copy-start(bf16[2048,192]{0,1:T(8,128)(2,1)} %copy.36) | copy-start | bytes 2359300
  137.6 40.4 %copy-start.14 = (f32[768]{0:T(1024)S(1)}, f32[768]{0:T(1024)}, u32[]{:S(2)}) copy-start(f32[768]{0:T(1024)} %param.21) | copy-start | bytes 9220
  137.6 69.0 %all-gather.6.cloned.1.call-start = ((), (), s32[]{:S(2)}) async-start(), calls=%async_computation.6 | async-start | bytes 3932160 | tf_op jit(solution)/shard_map/all_gather | solution.py:142
  177.9 126.5 %all-reduce.3.cloned.1.call-start = ((), (), s32[]{:S(2)}) async-start(), calls=%async_computation.7 | async-start | bytes 884736 | tf_op jit(solution)/shard_map/psum | solution.py:179
  214.9 4.2 %copy-start.2 = (bf16[8192,192]{0,1:T(8,128)(2,1)S(1)}, bf16[8192,192]{0,1:T(8,128)(2,1)}, u32[]{:S(2)}) copy-start(bf16[8192,192]{0,1:T(8,128)(2,1)} %all-gather.6.cloned.1.call-done) | copy-start | bytes 9437188
  219.9 1.2 copy-start.11
  220.5 1.4 copy-start.4
  222.6 0.8 copy-start.15
  224.0 1.0 copy-start.9
  234.1 76.6 %copy-start.5 = (f32[1,2,192,384]{3,2,1,0:T(8,128)S(1)}, f32[1,2,192,384]{3,2,1,0:T(8,128)}, u32[]{:S(2)}) copy-start(f32[1,2,192,384]{3,2,1,0:T(8,128)} %param.24) | copy-start | bytes 1769476
  234.1 76.6 %copy-start.7 = (bf16[2048,192]{0,1:T(8,128)(2,1)S(1)}, bf16[2048,192]{0,1:T(8,128)(2,1)}, u32[]{:S(2)}) copy-start(bf16[2048,192]{0,1:T(8,128)(2,1)} %add_convert_fusion) | copy-start | bytes 2359300
  234.1 76.6 %copy-start.8 = (bf16[2048,192]{0,1:T(8,128)(2,1)S(1)}, bf16[2048,192]{0,1:T(8,128)(2,1)}, u32[]{:S(2)}) copy-start(bf16[2048,192]{0,1:T(8,128)(2,1)} %convolution_convert_fusion.5) | copy-start | bytes 2359300
  234.1 76.6 %copy-start.10 = (f32[1,384,192]{1,2,0:T(8,128)S(1)}, f32[1,384,192]{1,2,0:T(8,128)}, u32[]{:S(2)}) copy-start(f32[1,384,192]{1,2,0:T(8,128)} %param.25) | copy-start | bytes 884740
  304.5 6.3 %copy-start.12 = (bf16[192,384]{1,0:T(8,128)(2,1)S(1)}, bf16[192,384]{1,0:T(8,128)(2,1)}, u32[]{:S(2)}) copy-start(bf16[192,384]{1,0:T(8,128)(2,1)} %get-tuple-element.95) | copy-start | bytes 442372
  304.5 6.3 %copy-start.13 = (bf16[384,192]{0,1:T(8,128)(2,1)S(1)}, bf16[384,192]{0,1:T(8,128)(2,1)}, u32[]{:S(2)}) copy-start(bf16[384,192]{0,1:T(8,128)(2,1)} %get-tuple-element.96) | copy-start | bytes 442372
  310.7 4.3 %copy-start.1 = (bf16[192,768]{1,0:T(8,128)(2,1)S(1)}, bf16[192,768]{1,0:T(8,128)(2,1)}, u32[]{:S(2)}) copy-start(bf16[192,768]{1,0:T(8,128)(2,1)} %param.20) | copy-start | bytes 884740
Sparse Core Ops, SparseCore 0:
  75.0 27.2 all-gather.3
  137.7 37.8 reduce-scatter.1
  178.1 28.4 all-gather.5
  231.5 72.8 all-reduce.2
